TPU v7x, 256 devices: a whole 4x4x8 slice. The times are simulated.
256 devices in a mesh: dp: 32 (over z, x_hi, core), mp: 8 (over x_lo, y).
Axes of the slice: x: 4 (x_hi: 2, x_lo: 2; x = x_hi * 2 + x_lo), y: 4, z: 8, core: 2. Of those that a mesh axis runs over, the one named last changes fastest.
Arguments:
- tokens: bfloat16 [1024, 16384], P('dp', 'mp'), may hold values from -6 to 6
- gate_weight: bfloat16 [16384, 28672], P('mp', 'dp'), may hold values from -0.046875 to 0.046875
- up_weight: bfloat16 [16384, 28672], P('mp', 'dp'), may hold values from -0.046875 to 0.046875
- down_weight: bfloat16 [28672, 16384], P('dp', 'mp'), may hold values from -0.03125 to 0.03125
Outputs:
- mixed: bfloat16 [1024, 16384], P('dp', 'mp')
All inputs are finite; a program needn't handle non-finite values.
Results may differ from a plain program's by a relative error of at most 0.0049.
Values may be sent and summed in bfloat16 or wider, within the bound.
A program may use at most 64 MiB of HBM per device.

v0:
```python
import jax
import jax.numpy as jnp
from jax import lax
from jax.sharding import PartitionSpec as P


def in_order(blocks, dim):
    blocks = jnp.moveaxis(blocks, 0, dim)
    shape = blocks.shape
    return blocks.reshape(*shape[:dim], shape[dim] * shape[dim + 1], *shape[dim + 2 :])


def sent_to_all(x, axis):
    copies = jnp.broadcast_to(x, (lax.axis_size(axis), *x.shape))
    return lax.all_to_all(copies, axis, split_axis=0, concat_axis=0, tiled=True)


def collect(x, axis, dim):
    return in_order(sent_to_all(x, axis), dim)


def per_device(tokens, gate_weight, up_weight, down_weight):
    width = gate_weight.shape[1]
    piece = lax.all_gather(tokens, "dp", axis=0, tiled=True)
    gate_part = jnp.dot(piece, gate_weight, preferred_element_type=jnp.float32)
    up_part = jnp.dot(piece, up_weight, preferred_element_type=jnp.float32)
    partial_both = jnp.concatenate([gate_part, up_part], axis=1)
    share = lax.psum_scatter(partial_both, "mp", scatter_dimension=0, tiled=True)
    own_rows = (jax.nn.silu(share[:, :width]) * share[:, width:]).astype(jnp.bfloat16)
    hidden = collect(own_rows, "mp", 0)
    mixed = lax.psum_scatter(
        jnp.dot(hidden, down_weight, preferred_element_type=jnp.float32),
        "dp",
        scatter_dimension=0,
        tiled=True,
    )
    return mixed.astype(jnp.bfloat16)


def solution(mesh):
    return jax.shard_map(
        per_device,
        mesh=mesh,
        in_specs=(P("dp", "mp"), P("mp", "dp"), P("mp", "dp"), P("dp", "mp")),
        out_specs=P("dp", "mp"),
        check_vma=False,
    )
```

profile of v0, /device:TPU:8, one launch (start us, length us, event | category | flops | bytes accessed | tf_op | source)
XLA Modules:
  0.0 394.5 jit_solution(867062498399786874)
XLA Ops:
  6.5 0.0 all-gather.2.cloned.1.call-start
  6.5 0.7 all-gather.2.cloned.1.call-update
  7.3 0.0 reduce-scatter.3.cloned.1.call-start
  7.3 92.3 %all-gather.2.cloned.1.call-done = bf16[1024,2048]{1,0:T(8,128)(2,1)} async-done(((bf16[32,2048]{1,0:T(8,128)(2,1)}), bf16[1024,2048]{1,0:T(8,128)(2,1)}) %all-gather.2.cloned.1.call-update) | async-done | bytes 4194320 | tf_op jit(solution)/shard_map/all_gather | solution.py:24
  99.6 0.0 copy-start
  99.6 0.0 copy-start.1
  99.6 7.1 %fusion.2 = f32[1024,896]{0,1:T(8,128)S(1)} fusion(bf16[1024,2048]{1,0:T(8,128)(2,1)} %all-gather.2.cloned.1.call-done, bf16[2048,896]{1,0:T(8,128)(2,1)} %param.6), kind=kOutput, calls=%fused_computation.4 | convolution fusion | flops 3758096384 | bytes 11534336 | tf_op jit(solution)/shard_map/dot_general | solution.py:26
  106.7 0.0 copy-done
  106.7 0.0 copy-done.1
  106.7 4.2 %fusion.1 = f32[1024,896]{0,1:T(8,128)S(1)} fusion(bf16[1024,2048]{1,0:T(8,128)(2,1)S(1)} %copy-done, bf16[2048,896]{1,0:T(8,128)(2,1)S(1)} %copy-done.1), kind=kOutput, calls=%fused_computation.3 | convolution fusion | flops 3758096384 | bytes 11534336 | tf_op jit(solution)/shard_map/dot_general | solution.py:25
  111.0 3.7 pad_maximum_fusion
  114.6 0.0 reduce-scatter.3.cloned.1.call-update
  114.6 0.0 reduce-scatter.5.cloned.1.call-start
  114.7 80.1 %reduce-scatter.3.cloned.1.call-done = f32[128,1792]{0,1:T(8,128)} async-done(((f32[1024,1792]{0,1:T(8,128)}), f32[128,1792]{0,1:T(8,128)}) %reduce-scatter.3.cloned.1.call-update) | async-done | bytes 917520 | tf_op jit(solution)/shard_map/reduce_scatter | solution.py:28
  194.8 1.3 fusion
  196.1 0.2 copy.5
  196.2 0.0 copy-start.2
  196.2 0.2 broadcast_in_dim.3
  196.5 28.2 %all_to_all.5 = bf16[8,128,896]{2,1,0:T(8,128)(2,1)S(1)} all-to-all(bf16[8,128,896]{2,1,0:T(8,128)(2,1)S(1)} %broadcast_in_dim.3), channel_id=1, replica_groups=mesh['dp'=32,'mp'=8] {'mp'}, dimensions={0} | all-to-all | bytes 3670016 | tf_op jit(solution)/shard_map/all_to_all | solution.py:15
  224.6 0.0 copy-done.2
  224.6 6.8 %fusion.3 = f32[1024,2048]{1,0:T(8,128)} fusion(bf16[1024,896]{1,0:T(8,128)(2,1)S(1)} %bitcast.7, bf16[896,2048]{1,0:T(8,128)(2,1)S(1)} %copy-done.2), kind=kOutput, calls=%fused_computation.5 | convolution fusion | flops 3758096384 | bytes 13893632 | tf_op jit(solution)/shard_map/dot_general | solution.py:32
  231.4 0.0 reduce-scatter.5.cloned.1.call-update
  231.4 154.9 %reduce-scatter.5.cloned.1.call-done = f32[32,2048]{1,0:T(8,128)} async-done(((f32[1024,2048]{1,0:T(8,128)}), f32[32,2048]{1,0:T(8,128)}) %reduce-scatter.5.cloned.1.call-update) | async-done | bytes 262160 | tf_op jit(solution)/shard_map/reduce_scatter | solution.py:31
  386.3 1.6 convert_element_type.7
Async XLA Ops:
  6.5 93.1 %all-gather.2.cloned.1.call-start = ((), (), s32[]{:S(2)}) async-start(), calls=%async_computation.3 | async-start | bytes 4325376 | tf_op jit(solution)/shard_map/all_gather | solution.py:24
  7.3 187.5 %reduce-scatter.3.cloned.1.call-start = ((), (), s32[]{:S(2)}) async-start(), calls=%async_computation.4 | async-start | bytes 8257536 | tf_op jit(solution)/shard_map/reduce_scatter | solution.py:28
  99.6 7.1 %copy-start = (bf16[1024,2048]{1,0:T(8,128)(2,1)S(1)}, bf16[1024,2048]{1,0:T(8,128)(2,1)}, u32[]{:S(2)}) copy-start(bf16[1024,2048]{1,0:T(8,128)(2,1)} %all-gather.2.cloned.1.call-done) | copy-start | bytes 12582916
  99.6 7.1 %copy-start.1 = (bf16[2048,896]{1,0:T(8,128)(2,1)S(1)}, bf16[2048,896]{1,0:T(8,128)(2,1)}, u32[]{:S(2)}) copy-start(bf16[2048,896]{1,0:T(8,128)(2,1)} %param.5) | copy-start | bytes 11010052
  114.6 271.7 %reduce-scatter.5.cloned.1.call-start = ((), (), s32[]{:S(2)}) async-start(), calls=%async_computation.5 | async-start | bytes 8650752 | tf_op jit(solution)/shard_map/reduce_scatter | solution.py:31
  196.2 28.4 %copy-start.2 = (bf16[896,2048]{1,0:T(8,128)(2,1)S(1)}, bf16[896,2048]{1,0:T(8,128)(2,1)}, u32[]{:S(2)}) copy-start(bf16[896,2048]{1,0:T(8,128)(2,1)} %param.7) | copy-start | bytes 11010052
Sparse Core Ops, SparseCore 0:
  10.1 89.4 all-gather.1
  114.8 79.9 reduce-scatter.2
  231.6 154.7 reduce-scatter.4
where the time goes:
time: 395 us; the launch traced here: 394 us
  waiting for transfers between devices  328 us (83%)
  blocking collectives  28.2 us (7%)
  matrix products  18.1 us (5%)
  between operations  13.2 us (3%)
  other arithmetic  6.57 us (2%)
    reduce_scatter x1, waiting for transfers between devices, per_device(): lax.psum_scatter(jnp.dot(hidden, down_weight, preferred_element_type=jnp....  155 us
    all_gather x1, waiting for transfers between devices, per_device(): piece = lax.all_gather(tokens, 'dp', axis=0, tiled=True)  92.3 us
    reduce_scatter x1, waiting for transfers between devices, per_device(): lax.psum_scatter(partial_both, 'mp', scatter_dimension=0, tiled=True)  80.1 us
    all_to_all x1, blocking collectives, sent_to_all(): return lax.all_to_all(copies, axis, split_axis=0, concat_axis=0, tiled=True)  28.2 us
  transfers between devices with their start and end apart: 3, of which 3 were waited for; matrix products, arithmetic and copies ran while one was open for 0% of the time, Pallas kernels for 0%

commit v1 on v0

--- a/solution.py
+++ b/solution.py
@@ -21,7 +21,10 @@
 
 def per_device(tokens, gate_weight, up_weight, down_weight):
     width = gate_weight.shape[1]
-    piece = lax.all_gather(tokens, "dp", axis=0, tiled=True)
+    inbox = []
+    for _ in range(lax.axis_size("dp")):
+        inbox.append(tokens)
+    piece = jnp.concatenate(lax.all_to_all(jnp.stack(inbox), "dp", 0, 0), axis=0)
     gate_part = jnp.dot(piece, gate_weight, preferred_element_type=jnp.float32)
     up_part = jnp.dot(piece, up_weight, preferred_element_type=jnp.float32)
     partial_both = jnp.concatenate([gate_part, up_part], axis=1)

time: 395 us -> 407 us (1.030)
  blocking collectives: 28.2 us -> 136 us
  waiting for transfers between devices: 328 us -> 235 us
    all_to_all x0 -> x1, blocking collectives: none -> 107 us  [per_device(): lax.all_to_all(jnp.stack(inbox), 'dp', 0, 0)]
    all_gather x1 -> x0, waiting for transfers between devices: 92.3 us -> none  [per_device(): piece = lax.all_gather(tokens, 'dp', axis=0, tiled=True)]
  transfers between devices with their start and end apart: 3 -> 2, of which waited for: 3 -> 2; matrix products, arithmetic and copies ran while one was open for 0% -> 0% of each run, Pallas kernels for 0% -> 0%
where the time goes in v1:
time: 407 us
  waiting for transfers between devices  235 us (58%)
  blocking collectives  136 us (33%)
  matrix products  15.1 us (4%)
  between operations  13.5 us (3%)
  other arithmetic  6.57 us (2%)
    reduce_scatter x1, waiting for transfers between devices, per_device(): lax.psum_scatter(jnp.dot(hidden, down_weight, preferred_element_type=jnp....  155 us
    all_to_all x1, blocking collectives, per_device(): lax.all_to_all(jnp.stack(inbox), 'dp', 0, 0)  107 us
    reduce_scatter x1, waiting for transfers between devices, per_device(): lax.psum_scatter(partial_both, 'mp', scatter_dimension=0, tiled=True)  80.2 us
    all_to_all x1, blocking collectives, sent_to_all(): return lax.all_to_all(copies, axis, split_axis=0, concat_axis=0, tiled=True)  28.2 us
  transfers between devices with their start and end apart: 2, of which 2 were waited for; matrix products, arithmetic and copies ran while one was open for 0% of the time, Pallas kernels for 0%

profile of v1, /device:TPU:8, one launch (start us, length us, event | category | flops | bytes accessed | tf_op | source)
XLA Modules:
  0.0 407.3 jit_solution(17564352064960186925)
XLA Ops:
  6.5 0.0 reduce-scatter.3.cloned.1.call-start
  6.5 1.4 stack.2
  8.0 0.0 copy-start
  8.0 107.4 %all_to_all.10 = bf16[32,32,2048]{2,1,0:T(8,128)(2,1)S(1)} all-to-all(bf16[32,32,2048]{2,1,0:T(8,128)(2,1)S(1)} %stack.2), channel_id=1, replica_groups=mesh['dp'=32,'mp'=8] {'dp'}, dimensions={0} | all-to-all | bytes 8388608 | tf_op jit(solution)/shard_map/all_to_all | solution.py:27
  115.3 0.0 copy-done
  115.3 0.0 copy-start.1
  115.3 4.2 %fusion.2 = f32[1024,896]{0,1:T(8,128)S(1)} fusion(bf16[1024,2048]{1,0:T(8,128)(2,1)S(1)} %bitcast.8, bf16[2048,896]{1,0:T(8,128)(2,1)S(1)} %copy-done), kind=kOutput, calls=%fused_computation.4 | convolution fusion | flops 3758096384 | bytes 11534336 | tf_op jit(solution)/shard_map/dot_general | solution.py:29
  119.6 0.0 copy-done.1
  119.6 4.2 %fusion.1 = f32[1024,896]{0,1:T(8,128)S(1)} fusion(bf16[1024,2048]{1,0:T(8,128)(2,1)S(1)} %bitcast.9, bf16[2048,896]{1,0:T(8,128)(2,1)S(1)} %copy-done.1), kind=kOutput, calls=%fused_computation.3 | convolution fusion | flops 3758096384 | bytes 11534336 | tf_op jit(solution)/shard_map/dot_general | solution.py:28
  123.8 3.7 pad_maximum_fusion
  127.5 0.0 reduce-scatter.3.cloned.1.call-update
  127.5 0.0 reduce-scatter.5.cloned.1.call-start
  127.6 80.2 %reduce-scatter.3.cloned.1.call-done = f32[128,1792]{0,1:T(8,128)} async-done(((f32[1024,1792]{0,1:T(8,128)}), f32[128,1792]{0,1:T(8,128)}) %reduce-scatter.3.cloned.1.call-update) | async-done | bytes 917520 | tf_op jit(solution)/shard_map/reduce_scatter | solution.py:31
  207.8 1.3 fusion
  209.1 0.2 copy.5
  209.2 0.0 copy-start.2
  209.2 0.2 broadcast_in_dim.3
  209.5 28.2 %all_to_all.11 = bf16[8,128,896]{2,1,0:T(8,128)(2,1)S(1)} all-to-all(bf16[8,128,896]{2,1,0:T(8,128)(2,1)S(1)} %broadcast_in_dim.3), channel_id=1, replica_groups=mesh['dp'=32,'mp'=8] {'mp'}, dimensions={0} | all-to-all | bytes 3670016 | tf_op jit(solution)/shard_map/all_to_all | solution.py:15
  237.6 0.0 copy-done.2
  237.6 6.6 %fusion.3 = f32[1024,2048]{1,0:T(8,128)} fusion(bf16[1024,896]{1,0:T(8,128)(2,1)S(1)} %bitcast.10, bf16[896,2048]{1,0:T(8,128)(2,1)S(1)} %copy-done.2), kind=kOutput, calls=%fused_computation.5 | convolution fusion | flops 3758096384 | bytes 13893632 | tf_op jit(solution)/shard_map/dot_general | solution.py:35
  244.3 0.0 reduce-scatter.5.cloned.1.call-update
  244.3 154.5 %reduce-scatter.5.cloned.1.call-done = f32[32,2048]{1,0:T(8,128)} async-done(((f32[1024,2048]{1,0:T(8,128)}), f32[32,2048]{1,0:T(8,128)}) %reduce-scatter.5.cloned.1.call-update) | async-done | bytes 262160 | tf_op jit(solution)/shard_map/reduce_scatter | solution.py:34
  398.8 1.6 convert_element_type.7
Async XLA Ops:
  6.5 201.2 %reduce-scatter.3.cloned.1.call-start = ((), (), s32[]{:S(2)}) async-start(), calls=%async_computation.4 | async-start | bytes 8257536 | tf_op jit(solution)/shard_map/reduce_scatter | solution.py:31
  8.0 107.4 %copy-start = (bf16[2048,896]{1,0:T(8,128)(2,1)S(1)}, bf16[2048,896]{1,0:T(8,128)(2,1)}, u32[]{:S(2)}) copy-start(bf16[2048,896]{1,0:T(8,128)(2,1)} %param.6) | copy-start | bytes 11010052
  115.3 4.2 %copy-start.1 = (bf16[2048,896]{1,0:T(8,128)(2,1)S(1)}, bf16[2048,896]{1,0:T(8,128)(2,1)}, u32[]{:S(2)}) copy-start(bf16[2048,896]{1,0:T(8,128)(2,1)} %param.5) | copy-start | bytes 11010052
  127.5 271.3 %reduce-scatter.5.cloned.1.call-start = ((), (), s32[]{:S(2)}) async-start(), calls=%async_computation.5 | async-start | bytes 8650752 | tf_op jit(solution)/shard_map/reduce_scatter | solution.py:34
  209.2 28.4 %copy-start.2 = (bf16[896,2048]{1,0:T(8,128)(2,1)S(1)}, bf16[896,2048]{1,0:T(8,128)(2,1)}, u32[]{:S(2)}) copy-start(bf16[896,2048]{1,0:T(8,128)(2,1)} %param.7) | copy-start | bytes 11010052
Sparse Core Ops, SparseCore 0:
  127.7 80.0 reduce-scatter.2
  244.4 154.3 reduce-scatter.4
